TPU v7x, 128 devices: a whole 4x4x4 slice. The times are simulated.
128 devices in a mesh: sec: 2 (over z_lo), tile: 64 (over y, z_hi, x, core).
Axes of the slice: x: 4, y: 4, z: 4 (z_hi: 2, z_lo: 2; z = z_hi * 2 + z_lo), core: 2. Of those that a mesh axis runs over, the one named last changes fastest.
Arguments:
- atmosphere: bfloat16 [128, 360, 384], P(('sec', 'tile')), may hold values from -6 to 6
- ocean_state: bfloat16 [512, 1440, 128], P('tile', 'sec'), may hold values from -6 to 6
- land_mask: int32 [512, 1440], P('tile', 'sec'), may hold values 0 or 1
- crossing_bands: int32 [64, 4], P('tile'), may hold values from 0 to 127, as said below
- ocean_regrid: float32 [64, 4, 8, 1], P('tile'), may hold values from 0 to 1, as said below
- atmosphere_regrid: float32 [64, 4, 1, 8], P('tile'), may hold values from 0 to 1, as said below
- surface_read: bfloat16 [128], replicated, may hold values from -0.5 to 0.5
- surface_embed: float32 [384], replicated, may hold values from -4 to 4
- flux_read: bfloat16 [384, 8], replicated, may hold values from -0.3125 to 0.3125
- flux_embed: bfloat16 [8, 128], replicated, may hold values from -2 to 2
- legendre_forward: bfloat16 [128, 128, 128], P(('sec', 'tile')), may hold values from -0.5 to 0.5
- legendre_inverse: bfloat16 [128, 128, 128], P(('sec', 'tile')), may hold values from -0.5 to 0.5
- spectral_mix: bfloat16 [2, 384, 384], replicated, may hold values from -0.3125 to 0.3125
- conv_kernel: bfloat16 [2, 7, 7, 128], replicated, may hold values from -0.875 to 0.875
- norm_gain: float32 [2, 128], replicated, may hold values from 0.1 to 1.9
- expand_weight: bfloat16 [2, 128, 512], replicated, may hold values from -0.5 to 0.5
- project_weight: bfloat16 [2, 512, 128], replicated, may hold values from -0.25 to 0.25
- atmosphere_cotangent: bfloat16 [128, 360, 384], P(('sec', 'tile')), may hold values from -6 to 6
- ocean_cotangent: bfloat16 [512, 1440, 128], P('tile', 'sec'), may hold values from -6 to 6
Outputs:
- atmosphere_next: bfloat16 [128, 360, 384], P(('sec', 'tile'))
- ocean_next: bfloat16 [512, 1440, 128], P('tile', 'sec')
- atmosphere_grad: float32 [128, 360, 384], P(('sec', 'tile'))
- ocean_grad: float32 [512, 1440, 128], P('tile', 'sec')
Inputs may be any that keep to these rules, and one draw needn't show every extreme that they name: `crossing_bands`: row j lists between 1 and 4 consecutive distinct atmosphere bands, then repeats its last band; some row lists 4. Its first band is j * 2 - 1, j * 2 or j * 2 + 1, raised to 0 or lowered as far as needed for the list to end at band 128 - 1 at most. `ocean_regrid`: zero in the repeated slots of crossing_bands; the entries of each ocean row sum to one. `atmosphere_regrid`: zero in the repeated slots of crossing_bands.
All inputs are finite; a program needn't handle non-finite values. No bound on the sum of `land_mask` on one device may be relied on, other than what follows from the above.
Results may differ from a plain program's by a relative error of at most 0.008.
Values may be sent and summed in bfloat16 or wider, within the bound.
A program may use at most 128 MiB of HBM per device.

v0:
```python
import jax
import jax.numpy as jnp
from jax import lax
from jax.sharding import Mesh
from jax.sharding import PartitionSpec as P

SEC_TILE = ("sec", "tile_0", "tile_1", "tile_2", "tile_3")
TILE = ("tile_0", "tile_1", "tile_2", "tile_3")


def in_blocks(x, dim, size):
    lengths = x.shape
    blocks = x.reshape(*lengths[:dim], size, lengths[dim] // size, *lengths[dim + 1 :])
    return jnp.moveaxis(blocks, dim, 0)


def laid_out(blocks, dim):
    lengths = list(blocks.shape[1:])
    lengths[dim] *= blocks.shape[0]
    return jnp.moveaxis(blocks, 0, dim).reshape(lengths)


def turned_blocks(blocks, axes, sequence):
    lengths = [lax.axis_size(a) for a in axes]
    blocks = blocks.reshape(*lengths, *blocks.shape[1:])
    for k in sequence:
        blocks = lax.all_to_all(blocks, axes[k], split_axis=k, concat_axis=k, tiled=True)
    return blocks.reshape(-1, *blocks.shape[len(axes) :])


def two_step_exchange(x, groups, sequence, split_dim, concat_dim):
    size = lax.axis_size(groups[0]) * lax.axis_size(groups[1])
    blocks = in_blocks(x, split_dim, size)
    return laid_out(turned_blocks(blocks, groups, sequence), concat_dim)


def with_halo(x, sides, width, wrap):
    for axis, dim in sides:
        size, length = (lax.axis_size(axis), x.shape[dim])
        up = [(i, (i + 1) % size) for i in range(size if wrap else size - 1)]
        down = [(j, i) for i, j in up]
        last = lax.slice_in_dim(x, length - width, length, axis=dim)
        first = lax.slice_in_dim(x, 0, width, axis=dim)
        before = lax.ppermute(last, axis, up)
        after = lax.ppermute(first, axis, down)
        x = jnp.concatenate([before, x, after], axis=dim)
    return x


def wave_table(lon_count, mode_count):
    longitude = jnp.arange(lon_count, dtype=jnp.int32)
    wavenumber = jnp.arange(mode_count, dtype=jnp.int32)
    phase = (longitude[:, None] * wavenumber[None, :] % lon_count).astype(jnp.float32) * (
        2.0 * jnp.pi / lon_count
    )
    scaled = jnp.stack([jnp.cos(phase), -jnp.sin(phase)], axis=2) * jnp.sqrt(
        jnp.float32(2.0 / lon_count)
    )
    return scaled.reshape(lon_count, 2 * mode_count).astype(jnp.bfloat16)


def depthwise(window, kernel):
    radius = kernel.shape[0] // 2
    height = window.shape[0] - 2 * radius
    extent = window.shape[1] - 2 * radius
    wide = window.astype(jnp.float32)
    weights = kernel.astype(jnp.float32)
    total = jnp.zeros((height, extent, window.shape[2]), jnp.float32)
    for shift_row in range(kernel.shape[0]):
        for shift_col in range(kernel.shape[1]):
            total = (
                total
                + wide[shift_row : shift_row + height, shift_col : shift_col + extent]
                * weights[shift_row, shift_col]
            )
    return total


def cell_forward(hidden, gain, expand, project):
    center = hidden - jnp.mean(hidden, axis=-1, keepdims=True)
    inverse_std = lax.rsqrt(jnp.mean(center * center, axis=-1, keepdims=True) + 1e-06)
    normed = (center * inverse_std * gain).astype(jnp.bfloat16)
    before = jnp.dot(normed, expand, preferred_element_type=jnp.float32)
    active = jax.nn.gelu(before).astype(jnp.bfloat16)
    return jnp.dot(active, project, preferred_element_type=jnp.float32)


def cell_backward(hidden, gain, expand, project, mask_value, cotangent):
    center = hidden - jnp.mean(hidden, axis=-1, keepdims=True)
    inverse_std = lax.rsqrt(jnp.mean(center * center, axis=-1, keepdims=True) + 1e-06)
    unit = center * inverse_std
    normed = (unit * gain).astype(jnp.bfloat16)
    before = jnp.dot(normed, expand, preferred_element_type=jnp.float32)
    masked = (mask_value[:, :, None] * cotangent).astype(jnp.bfloat16)
    active_adjoint = jnp.dot(masked, project.T, preferred_element_type=jnp.float32)
    _, gelu_back = jax.vjp(jax.nn.gelu, before)
    before_adjoint = gelu_back(active_adjoint)[0].astype(jnp.bfloat16)
    normed_adjoint = jnp.dot(before_adjoint, expand.T, preferred_element_type=jnp.float32)
    scaled = normed_adjoint * gain
    result = inverse_std * (
        scaled
        - jnp.mean(scaled, axis=-1, keepdims=True)
        - unit * jnp.mean(scaled * unit, axis=-1, keepdims=True)
    )
    return result.astype(jnp.bfloat16)


def ocean_matrix(bands_row, blocks, lat_count):
    lat_band = blocks.shape[2]
    index = bands_row[:, None] * lat_band + jnp.arange(lat_band, dtype=jnp.int32)[None, :]
    onehot = (index[:, :, None] == jnp.arange(lat_count, dtype=jnp.int32)[None, None, :]).astype(
        jnp.float32
    )
    return jnp.einsum("poi,pia->oa", blocks, onehot, precision=lax.Precision.HIGHEST)


def atmosphere_matrix(bands_row, blocks, lat_count):
    lat_band = blocks.shape[1]
    index = bands_row[:, None] * lat_band + jnp.arange(lat_band, dtype=jnp.int32)[None, :]
    onehot = (index[:, :, None] == jnp.arange(lat_count, dtype=jnp.int32)[None, None, :]).astype(
        jnp.float32
    )
    return jnp.einsum("pio,pia->ao", blocks, onehot, precision=lax.Precision.HIGHEST)


def mix_complex(coefficient, mix_real, mix_imag):
    real_part = coefficient[:, :, 0]
    imag_part = coefficient[:, :, 1]
    out_real = jnp.einsum(
        "lmc,cd->lmd", real_part, mix_real, preferred_element_type=jnp.float32
    ) - jnp.einsum("lmc,cd->lmd", imag_part, mix_imag, preferred_element_type=jnp.float32)
    out_imag = jnp.einsum(
        "lmc,cd->lmd", imag_part, mix_real, preferred_element_type=jnp.float32
    ) + jnp.einsum("lmc,cd->lmd", real_part, mix_imag, preferred_element_type=jnp.float32)
    return jnp.stack([out_real, out_imag], axis=2).astype(jnp.bfloat16)


def spectral_block(spectrum, forward, inverse, mixing):
    lat_count, columns, channels = spectrum.shape
    split = spectrum.reshape(lat_count, columns // 2, 2, channels)
    coefficient = jnp.einsum(
        "mla,amrc->lmrc", forward, split, preferred_element_type=jnp.float32
    ).astype(jnp.bfloat16)
    mixed = mix_complex(coefficient, mixing[0], mixing[1])
    returned = jnp.einsum(
        "mal,lmrc->amrc", inverse, mixed, preferred_element_type=jnp.float32
    ).astype(jnp.bfloat16)
    return returned.reshape(lat_count, columns, channels)


def spectral_adjoint(returned_adjoint, forward, inverse, mixing):
    lat_count, columns, channels = returned_adjoint.shape
    split = returned_adjoint.reshape(lat_count, columns // 2, 2, channels)
    mixed_adjoint = jnp.einsum(
        "mal,amrc->lmrc", inverse, split, preferred_element_type=jnp.float32
    ).astype(jnp.bfloat16)
    real_part = mixed_adjoint[:, :, 0]
    imag_part = mixed_adjoint[:, :, 1]
    back_real = jnp.einsum(
        "lmd,cd->lmc", real_part, mixing[0], preferred_element_type=jnp.float32
    ) + jnp.einsum("lmd,cd->lmc", imag_part, mixing[1], preferred_element_type=jnp.float32)
    back_imag = jnp.einsum(
        "lmd,cd->lmc", imag_part, mixing[0], preferred_element_type=jnp.float32
    ) - jnp.einsum("lmd,cd->lmc", real_part, mixing[1], preferred_element_type=jnp.float32)
    coefficient_adjoint = jnp.stack([back_real, back_imag], axis=2).astype(jnp.bfloat16)
    spectrum_adjoint = jnp.einsum(
        "mla,lmrc->amrc", forward, coefficient_adjoint, preferred_element_type=jnp.float32
    ).astype(jnp.bfloat16)
    return spectrum_adjoint.reshape(lat_count, columns, channels)


def to_modes(values):
    return two_step_exchange(
        values, (("sec", "tile_0", "tile_1", "tile_2"), "tile_3"), (1, 0), 1, 0
    )


def to_bands(values):
    return lax.all_to_all(values, SEC_TILE, split_axis=0, concat_axis=1, tiled=True)


def rims(values, width):
    with_rows = with_halo(values, ((TILE, 0),), width, False)
    return with_halo(with_rows, (("sec", 1),), width, True)


def spread_rows(matrix, values):
    return lax.psum_scatter(
        jnp.dot(matrix, values, precision=lax.Precision.HIGHEST),
        SEC_TILE,
        scatter_dimension=0,
        tiled=True,
    )


def collect_rows(matrix, values, lon_count, fields, offset, half):
    piece = lax.all_gather(values, SEC_TILE, axis=0, tiled=True)
    own = lax.dynamic_slice_in_dim(
        piece.reshape(piece.shape[0], lon_count, fields), offset, half, 1
    )
    return jnp.dot(
        matrix, own.reshape(piece.shape[0], half * fields), precision=lax.Precision.HIGHEST
    )


def place_half(values, lon_count, offset):
    shape = (values.shape[0], lon_count) + values.shape[2:]
    empty = jnp.zeros(shape, jnp.float32)
    starts = (jnp.int32(0), offset) + tuple((jnp.int32(0) for extra in values.shape[2:]))
    return lax.dynamic_update_slice(empty, values, starts)


def per_device(
    atmosphere,
    ocean_state,
    land_mask,
    crossing_bands,
    ocean_regrid,
    atmosphere_regrid,
    surface_read,
    surface_embed,
    flux_read,
    flux_embed,
    legendre_forward,
    legendre_inverse,
    spectral_mix,
    conv_kernel,
    norm_gain,
    expand_weight,
    project_weight,
    atmosphere_cotangent,
    ocean_cotangent,
):
    band_total = lax.axis_size(SEC_TILE)
    lat_rows, lon_count, channels = atmosphere.shape
    lat_count = lat_rows * band_total
    ocean_rows, ocean_lon, ocean_channels = ocean_state.shape
    half = lon_count // lax.axis_size("sec")
    offset = lax.axis_index("sec") * half
    ratio = ocean_lon // half
    flux_count = flux_read.shape[1]
    radius = conv_kernel.shape[1] // 2
    layer_count = conv_kernel.shape[0]
    highest = lax.Precision.HIGHEST
    mask_value = land_mask.astype(jnp.float32)
    to_ocean = ocean_matrix(crossing_bands[0], ocean_regrid[0], lat_count)
    to_atmosphere = atmosphere_matrix(crossing_bands[0], atmosphere_regrid[0], lat_count)
    surface = jnp.dot(ocean_state, surface_read, preferred_element_type=jnp.float32)
    coarse = jnp.mean((mask_value * surface).reshape(ocean_rows, half, ratio), axis=2)
    surface_atmosphere = spread_rows(to_atmosphere, place_half(coarse, lon_count, offset))
    flux = jnp.einsum("agc,cf->agf", atmosphere, flux_read, preferred_element_type=jnp.float32)
    flux_ocean = collect_rows(
        to_ocean,
        flux.reshape(lat_rows, lon_count * flux_count),
        lon_count,
        flux_count,
        offset,
        half,
    )
    mixed_input = (
        atmosphere.astype(jnp.float32)
        + surface_atmosphere[:, :, None] * surface_embed[None, None, :]
    ).astype(jnp.bfloat16)
    table = wave_table(lon_count, legendre_forward.shape[0] * band_total)
    spectrum = jnp.einsum(
        "gk,agc->akc", table, mixed_input, preferred_element_type=jnp.float32
    ).astype(jnp.bfloat16)
    returned = to_bands(
        spectral_block(to_modes(spectrum), legendre_forward, legendre_inverse, spectral_mix)
    )
    response = jnp.einsum("gk,akc->agc", table, returned, preferred_element_type=jnp.float32)
    atmosphere_next = (mixed_input.astype(jnp.float32) + jax.nn.gelu(response)).astype(jnp.bfloat16)
    forcing_coarse = jnp.einsum(
        "ogf,fc->ogc",
        flux_ocean.reshape(ocean_rows, half, flux_count),
        flux_embed.astype(jnp.float32),
        precision=highest,
    )
    forcing = jnp.broadcast_to(
        forcing_coarse[:, :, None, :], (ocean_rows, half, ratio, ocean_channels)
    ).reshape(ocean_rows, ocean_lon, ocean_channels)
    state = (ocean_state.astype(jnp.float32) + mask_value[:, :, None] * forcing).astype(
        jnp.bfloat16
    )
    windows = []
    for layer in range(layer_count):
        window = rims(state, radius)
        windows.append(window)
        update = cell_forward(
            depthwise(window, conv_kernel[layer]),
            norm_gain[layer],
            expand_weight[layer],
            project_weight[layer],
        )
        state = (state.astype(jnp.float32) + mask_value[:, :, None] * update).astype(jnp.bfloat16)
    cotangent = ocean_cotangent.astype(jnp.float32)
    for layer in range(layer_count - 1, -1, -1):
        hidden = depthwise(windows[layer], conv_kernel[layer])
        hidden_adjoint = cell_backward(
            hidden,
            norm_gain[layer],
            expand_weight[layer],
            project_weight[layer],
            mask_value,
            cotangent,
        )
        cotangent = cotangent + depthwise(
            rims(hidden_adjoint, radius), conv_kernel[layer, ::-1, ::-1]
        )
    forcing_adjoint = (
        (mask_value[:, :, None] * cotangent)
        .reshape(ocean_rows, half, ratio, ocean_channels)
        .sum(axis=2)
    )
    flux_ocean_adjoint = jnp.einsum(
        "ogc,fc->ogf", forcing_adjoint, flux_embed.astype(jnp.float32), precision=highest
    )
    full_adjoint = place_half(flux_ocean_adjoint, lon_count, offset)
    flux_adjoint = spread_rows(to_ocean.T, full_adjoint.reshape(ocean_rows, lon_count * flux_count))
    flux_adjoint = flux_adjoint.reshape(lat_rows, lon_count, flux_count)
    from_flux = jnp.einsum(
        "agf,cf->agc", flux_adjoint, flux_read.astype(jnp.float32), precision=highest
    )
    atmosphere_adjoint = atmosphere_cotangent.astype(jnp.float32)
    _, gelu_back = jax.vjp(jax.nn.gelu, response)
    response_adjoint = gelu_back(atmosphere_adjoint)[0].astype(jnp.bfloat16)
    returned_adjoint = jnp.einsum(
        "gk,agc->akc", table, response_adjoint, preferred_element_type=jnp.float32
    ).astype(jnp.bfloat16)
    spectrum_adjoint = to_bands(
        spectral_adjoint(
            to_modes(returned_adjoint), legendre_forward, legendre_inverse, spectral_mix
        )
    )
    input_adjoint = atmosphere_adjoint + jnp.einsum(
        "gk,akc->agc", table, spectrum_adjoint, preferred_element_type=jnp.float32
    )
    atmosphere_grad = input_adjoint + from_flux
    surface_adjoint = jnp.einsum("agc,c->ag", input_adjoint, surface_embed, precision=highest)
    coarse_adjoint = collect_rows(to_atmosphere.T, surface_adjoint, lon_count, 1, offset, half)
    widened_adjoint = jnp.broadcast_to(
        coarse_adjoint[:, :, None], (ocean_rows, half, ratio)
    ).reshape(ocean_rows, ocean_lon)
    surface_grad = mask_value * widened_adjoint / ratio
    ocean_grad = (
        cotangent + surface_grad[:, :, None] * surface_read.astype(jnp.float32)[None, None, :]
    )
    return (atmosphere_next, state, atmosphere_grad, ocean_grad)


def solution(mesh):
    finer = Mesh(
        mesh.devices.reshape(mesh.shape["sec"], 4, 2, 4, 2),
        ("sec", "tile_0", "tile_1", "tile_2", "tile_3"),
    )
    placed = (
        P(SEC_TILE, None, None),
        P(TILE, "sec", None),
        P(TILE, "sec"),
        P(TILE, None),
        P(TILE, None, None, None),
        P(TILE, None, None, None),
        P(),
        P(),
        P(),
        P(),
        P(SEC_TILE, None, None),
        P(SEC_TILE, None, None),
        P(),
        P(),
        P(),
        P(),
        P(),
        P(SEC_TILE, None, None),
        P(TILE, "sec", None),
    )
    return jax.shard_map(
        per_device,
        mesh=finer,
        in_specs=placed,
        out_specs=(
            P(SEC_TILE, None, None),
            P(TILE, "sec", None),
            P(SEC_TILE, None, None),
            P(TILE, "sec", None),
        ),
        check_vma=False,
    )
```

profile of v0, /device:TPU:1, one launch (start us, length us, event | category | flops | bytes accessed | tf_op | source)
XLA Modules:
  0.0 916.0 jit_solution(4656370942096807728)
XLA Ops:
  20.9 140.1 %all-reduce.8.cloned.1.call-done = f32[128,360]{1,0:T(8,128)} async-done(((f32[128,360]{1,0:T(8,128)}), f32[128,360]{1,0:T(8,128)}) %all-reduce.8.cloned.1.call-update) | async-done | bytes 184336
  162.3 4.5 all_to_all.38
  167.6 6.6 all-to-all-start.1
  174.8 8.5 all-to-all-done.1
  183.5 173.7 %all-gather.4.cloned.1.call-done = f32[128,1,2880]{2,1,0:T(1,128)} async-done(((f32[1,1,2880]{2,1,0:T(1,128)}), f32[128,1,2880]{2,1,0:T(1,128)}) %all-gather.4.cloned.1.call-update) | async-done | bytes 1474576 | tf_op jit(solution)/shard_map/all_gather | solution.py:197
  357.2 3.8 copy.78
  374.7 4.4 collective-permute-done.1
  381.7 13.4 %all-to-all-start.2 = ((bf16[128,2,384]{2,1,0:T(2,128)(2,1)}), bf16[128,2,384]{2,1,0:T(2,128)(2,1)}, u32[]{:S(2)}, u32[]{:S(2)}) async-start(bf16[128,2,384]{2,1,0:T(2,128)(2,1)} %copy.75), calls=%async_computation.2 | async-start | bytes 393216 | tf_op jit(solution)/shard_map/all_to_all | solution.py:179
  397.1 20.6 %fusion.376 = (f32[8,720]{1,0:T(8,128)S(1)}, f32[8,720,128]{2,1,0:T(8,128)S(1)}) fusion(f32[128]{0:T(128)S(1)} %get-tuple-element.184, f32[14,726,128]{2,1,0:T(8,128)S(1)} %maximum_convert_fusion, f32[128]{0:T(128)S(1)} %get-tuple-element.185, f32[128]{0:T(128)S(1)} %get-tuple-element.186, f32[128]{0:T(128)S(1)} %get-tuple-element.187, ...), kind=kLoop, calls=%fused_computation.842 | loop fusion | flops 72247680 | bytes 147504128 | tf_op jit(solution)/shard_map/reduce_sum | solution.py:80
  422.0 4.9 add_convert_fusion.1
  428.4 3.5 collective-permute-start.4
  441.2 3.5 all_to_all.39
  445.5 12.4 %all-to-all-start.4 = ((bf16[64,2,1,2,384]{4,3,1,2,0:T(2,128)(2,1)}), bf16[64,2,1,2,384]{4,3,1,2,0:T(2,128)(2,1)}, u32[]{:S(2)}, u32[]{:S(2)}) async-start(bf16[64,2,1,2,384]{4,3,1,2,0:T(2,128)(2,1)} %copy.84), calls=%async_computation.4 | async-start | bytes 393216 | tf_op jit(solution)/shard_map/all_to_all | solution.py:27
  463.2 3.6 all-to-all-done.4
  472.6 20.5 %fusion.374 = (f32[8,720]{1,0:T(8,128)S(1)}, f32[8,720,128]{2,1,0:T(8,128)S(1)}) fusion(f32[128]{0:T(128)S(1)} %copy-done.101, f32[14,726,128]{2,1,0:T(8,128)S(1)} %maximum_convert_fusion.1, f32[128]{0:T(128)S(1)} %copy-done.102, f32[128]{0:T(128)S(1)} %copy-done.103, f32[128]{0:T(128)S(1)} %copy-done.104, f32[128]{0:T(128)S(1)} %copy-done.105, ...), kind=kLoop, calls=%fused_computation.841 | loop fusion | flops 72247680 | bytes 147504128 | tf_op jit(solution)/shard_map/reduce_sum | solution.py:80
  495.0 5.4 fusion.219
  500.4 15.5 %multiply_reduce_fusion.5 = (f32[8,720]{1,0:T(8,128)S(1)}, f32[8,720]{1,0:T(8,128)S(1)}, f32[8,720,128]{2,1,0:T(8,128)}) fusion(f32[128]{0:T(128)S(1)} %copy-done.44, f32[8,720]{1,0:T(8,128)S(1)} %add_rsqrt_fusion, f32[8,720,128]{2,1,0:T(8,128)} %copy-done.2, f32[8,720]{1,0:T(8,128)S(1)} %broadcast_multiply_fusion.6, ...), kind=kOutput, calls=%fused_computation.438 | convolution fusion | flops 1575555840 | bytes 19551744 | tf_op jit(solution)/shard_map/dot_general | solution.py:98
  515.9 6.9 multiply_convert_fusion.6
  522.9 3.8 collective-permute-start.8
  529.5 3.7 collective-permute-done.8
  533.2 4.4 collective-permute-done.9
  541.3 3.5 maximum_convert_fusion.2
  545.1 64.0 %convert_add_fusion = f32[8,720,128]{2,1,0:T(8,128)} fusion(bf16[8,720,128]{2,1,0:T(8,128)(2,1)S(1)} %copy-done.15, f32[14,726,128]{2,1,0:T(8,128)} %maximum_convert_fusion.2, f32[128]{0:T(128)S(1)} %copy-done.54, f32[128]{0:T(128)S(1)} %copy-done.55, f32[128]{0:T(128)S(1)} %copy-done.56, f32[128]{0:T(128)S(1)} %copy-done.57, f32[128]{0:T(128)S(1)} %copy-done.58, ...), kind=kLoop, calls=%fused_computation.26 | loop fusion | flops 72990720 | bytes 148955648 | tf_op jit(solution)/shard_map/add | solution.py:307
  609.2 13.6 %multiply_reduce_fusion.4 = (f32[8,720]{1,0:T(8,128)S(1)}, f32[8,720]{1,0:T(8,128)S(1)}, f32[8,720,128]{2,1,0:T(8,128)}) fusion(f32[128]{0:T(128)S(1)} %copy-done.43, f32[8,720]{1,0:T(8,128)S(1)} %copy-done.24, f32[8,720,128]{2,1,0:T(8,128)S(1)} %get-tuple-element.17, f32[8,720]{1,0:T(8,128)S(1)} %copy-done.17, bf16[2,128,512]{2,1,0:T(8,128)(2,1)S(1)} %copy-done.20, ...), kind=kOutput, calls=%fused_computation.437 | convolution fusion | flops 1574818560 | bytes 21026304 | tf_op jit(solution)/shard_map/dot_general | solution.py:98
  622.7 7.0 multiply_convert_fusion.4
  638.2 13.8 %all-to-all-start.5 = ((bf16[128,2,384]{2,1,0:T(2,128)(2,1)}), bf16[128,2,384]{2,1,0:T(2,128)(2,1)}, u32[]{:S(2)}, u32[]{:S(2)}) async-start(bf16[128,2,384]{2,1,0:T(2,128)(2,1)} %copy.87), calls=%async_computation.5 | async-start | bytes 393216 | tf_op jit(solution)/shard_map/all_to_all | solution.py:179
  653.8 8.3 all-to-all-done.5
  670.4 59.1 %broadcast_multiply_fusion = (f32[8,720,128]{2,1,0:T(8,128)}, f32[8,720,128]{2,1,0:T(8,128)S(1)}) fusion(f32[8,720]{1,0:T(8,128)S(1)} %copy-done.27, f32[8,720,128]{2,1,0:T(8,128)} %convert_add_fusion, f32[128]{0:T(128)S(1)} %copy-done.47, f32[14,726,128]{2,1,0:T(8,128)} %maximum_convert_fusion.3, f32[128]{0:T(128)S(1)} %copy-done.48, ...), kind=kLoop, calls=%fused_computation.447 | loop fusion | flops 72990720 | bytes 153402368 | tf_op jit(solution)/shard_map/mul | solution.py:311
  729.5 4.5 reduce_sum.115
  737.6 5.0 dynamic_update_slice.7
  748.5 8.4 add_convert_fusion
  756.9 140.1 %all-reduce.10.cloned.1.call-done = (f32[128,2880]{1,0:T(8,128)}, f32[128,360]{1,0:T(8,128)}) async-done(((f32[128,2880]{1,0:T(8,128)}, f32[128,360]{1,0:T(8,128)}), (f32[128,2880]{1,0:T(8,128)}, f32[128,360]{1,0:T(8,128)})) %all-reduce.10.cloned.1.call-update) | async-done | bytes 1658896
  (410 shorter events, 108.3 us)
Async XLA Ops:
  7.2 373.5 %copy-start = (bf16[1,128,128]{2,1,0:T(8,128)(2,1)S(1)}, bf16[1,128,128]{2,1,0:T(8,128)(2,1)}, u32[]{:S(2)}) copy-start(bf16[1,128,128]{2,1,0:T(8,128)(2,1)} %param.30) | copy-start | bytes 98308
  7.2 153.8 %all-reduce.8.cloned.1.call-start = ((), (), s32[]{:S(2)}) async-start(), calls=%async_computation.7 | async-start | bytes 393216
  13.4 169.9 %copy-start.29 = (bf16[1,128,128]{2,1,0:T(8,128)(2,1)S(1)}, bf16[1,128,128]{2,1,0:T(8,128)(2,1)}, u32[]{:S(2)}) copy-start(bf16[1,128,128]{2,1,0:T(8,128)(2,1)} %param.29) | copy-start | bytes 98308
  13.4 343.8 %all-gather.4.cloned.1.call-start = ((), (), s32[]{:S(2)}) async-start(), calls=%async_computation.6 | async-start | bytes 1519104 | tf_op jit(solution)/shard_map/all_gather | solution.py:197
  14.5 407.5 %copy-start.25 = (f32[8,720]{1,0:T(8,128)}, f32[8,720]{1,0:T(8,128)S(1)}, u32[]{:S(2)}) copy-start(f32[8,720]{1,0:T(8,128)S(1)} %convert_element_type.219) | copy-start | bytes 69124
  16.1 167.4 %copy-start.13 = (bf16[360,128,2]{1,0,2:T(8,128)(2,1)}, bf16[360,128,2]{1,0,2:T(8,128)(2,1)S(1)}, u32[]{:S(2)}) copy-start(bf16[360,128,2]{1,0,2:T(8,128)(2,1)S(1)} %fusion.261) | copy-start | bytes 552964
  16.5 167.0 %copy-start.28 = (bf16[360,256]{0,1:T(8,128)(2,1)}, bf16[360,256]{0,1:T(8,128)(2,1)S(1)}, u32[]{:S(2)}) copy-start(bf16[360,256]{0,1:T(8,128)(2,1)S(1)} %convert_element_type.224) | copy-start | bytes 552964
  16.7 344.4 %copy-start.38 = (f32[128,8]{0,1:T(8,128)}, f32[128,8]{0,1:T(8,128)S(1)}, u32[]{:S(2)}) copy-start(f32[128,8]{0,1:T(8,128)S(1)} %fusion.336) | copy-start | bytes 12292
  19.5 341.5 %copy-start.31 = (f32[7,7,128]{2,1,0:T(8,128)}, f32[7,7,128]{2,1,0:T(8,128)S(1)}, u32[]{:S(2)}) copy-start(f32[7,7,128]{2,1,0:T(8,128)S(1)} %bitcast_convert_fusion) | copy-start | bytes 75268
  167.6 15.6 %all-to-all-start.1 = ((bf16[64,2,1,2,384]{4,3,1,2,0:T(2,128)(2,1)}), bf16[64,2,1,2,384]{4,3,1,2,0:T(2,128)(2,1)S(1)}, u32[]{:S(2)}, u32[]{:S(2)}) async-start(bf16[64,2,1,2,384]{4,3,1,2,0:T(2,128)(2,1)} %copy.72), calls=%async_computation.1 | async-start | bytes 393216 | tf_op jit(solution)/shard_map/all_to_all | solution.py:27
  174.2 188.2 %copy-start.40 = (bf16[8,128]{1,0:T(8,128)(2,1)S(1)}, bf16[8,128]{1,0:T(8,128)(2,1)}, u32[]{:S(2)}) copy-start(bf16[8,128]{1,0:T(8,128)(2,1)} %param.28) | copy-start | bytes 6148
  174.8 244.9 %copy-start.42 = (f32[128]{0:T(128)}, f32[128]{0:T(128)S(1)}, u32[]{:S(2)}) copy-start(f32[128]{0:T(128)S(1)} %get-tuple-element.235) | copy-start | bytes 1540
  364.9 9.8 %collective-permute-start = (bf16[3,720,128]{2,1,0:T(8,128)(2,1)S(1)}, bf16[3,720,128]{2,1,0:T(8,128)(2,1)S(1)}, u32[]{:S(2)}, u32[]{:S(2)}) collective-permute-start(bf16[3,720,128]{2,1,0:T(8,128)(2,1)S(1)} %get-tuple-element.34), channel_id=1, source_target_pairs={{0,1},{1,2},{2,3},{3,4},{4,5},{5,6},{6,7},{7,8},{8,9},{9,10},{10,1... | collective-permute-start | bytes 1658888 | tf_op jit(solution)/shard_map/ppermute | solution.py:44
  368.3 10.8 %collective-permute-start.1 = (bf16[3,720,128]{2,1,0:T(8,128)(2,1)S(1)}, bf16[3,720,128]{2,1,0:T(8,128)(2,1)S(1)}, u32[]{:S(2)}, u32[]{:S(2)}) collective-permute-start(bf16[3,720,128]{2,1,0:T(8,128)(2,1)S(1)} %get-tuple-element.35), channel_id=1, source_target_pairs={{1,0},{2,1},{3,2},{4,3},{5,4},{6,5},{7,6},{8,7},{9,8},{10,9},{11,1... | collective-permute-start | bytes 1658888 | tf_op jit(solution)/shard_map/ppermute | solution.py:45
  379.1 16.0 %collective-permute-start.2 = (bf16[14,3,128]{2,1,0:T(4,128)(2,1)S(1)}, bf16[14,3,128]{2,1,0:T(4,128)(2,1)S(1)}, u32[]{:S(2)}, u32[]{:S(2)}) collective-permute-start(bf16[14,3,128]{2,1,0:T(4,128)(2,1)S(1)} %get-tuple-element.26), channel_id=1, source_target_pairs={{0,64},{64,0},{1,65},{65,1},{2,66},{66,2},{3,67},{67,3},{4,68},{68... | collective-permute-start | bytes 32264 | tf_op jit(solution)/shard_map/ppermute | solution.py:44
  380.4 14.7 %collective-permute-start.3 = (bf16[14,3,128]{2,1,0:T(4,128)(2,1)S(1)}, bf16[14,3,128]{2,1,0:T(4,128)(2,1)S(1)}, u32[]{:S(2)}, u32[]{:S(2)}) collective-permute-start(bf16[14,3,128]{2,1,0:T(4,128)(2,1)S(1)} %get-tuple-element.27), channel_id=1, source_target_pairs={{64,0},{0,64},{65,1},{1,65},{66,2},{2,66},{67,3},{3,67},{68,4},{4,... | collective-permute-start | bytes 32264 | tf_op jit(solution)/shard_map/ppermute | solution.py:45
  381.7 52.2 %all-to-all-start.2 = ((bf16[128,2,384]{2,1,0:T(2,128)(2,1)}), bf16[128,2,384]{2,1,0:T(2,128)(2,1)}, u32[]{:S(2)}, u32[]{:S(2)}) async-start(bf16[128,2,384]{2,1,0:T(2,128)(2,1)} %copy.75), calls=%async_computation.2 | async-start | bytes 393216 | tf_op jit(solution)/shard_map/all_to_all | solution.py:179
  428.4 31.6 %collective-permute-start.4 = (bf16[3,720,128]{2,1,0:T(8,128)(2,1)}, bf16[3,720,128]{2,1,0:T(8,128)(2,1)S(1)}, u32[]{:S(2)}, u32[]{:S(2)}) collective-permute-start(bf16[3,720,128]{2,1,0:T(8,128)(2,1)} %get-tuple-element.32), channel_id=1, source_target_pairs={{0,1},{1,2},{2,3},{3,4},{4,5},{5,6},{6,7},{7,8},{8,9},{9,10},{10,1... | collective-permute-start | bytes 1658888 | tf_op jit(solution)/shard_map/ppermute | solution.py:44
  432.0 28.0 %collective-permute-start.5 = (bf16[3,720,128]{2,1,0:T(8,128)(2,1)}, bf16[3,720,128]{2,1,0:T(8,128)(2,1)}, u32[]{:S(2)}, u32[]{:S(2)}) collective-permute-start(bf16[3,720,128]{2,1,0:T(8,128)(2,1)} %get-tuple-element.33), channel_id=1, source_target_pairs={{1,0},{2,1},{3,2},{4,3},{5,4},{6,5},{7,6},{8,7},{9,8},{10,9},{11,1... | collective-permute-start | bytes 1658888 | tf_op jit(solution)/shard_map/ppermute | solution.py:45
  445.5 21.3 %all-to-all-start.4 = ((bf16[64,2,1,2,384]{4,3,1,2,0:T(2,128)(2,1)}), bf16[64,2,1,2,384]{4,3,1,2,0:T(2,128)(2,1)}, u32[]{:S(2)}, u32[]{:S(2)}) async-start(bf16[64,2,1,2,384]{4,3,1,2,0:T(2,128)(2,1)} %copy.84), calls=%async_computation.4 | async-start | bytes 393216 | tf_op jit(solution)/shard_map/all_to_all | solution.py:27
  461.4 7.7 collective-permute-start.6
  462.4 6.6 collective-permute-start.7
  522.9 10.3 %collective-permute-start.8 = (bf16[3,720,128]{2,1,0:T(8,128)(2,1)S(1)}, bf16[3,720,128]{2,1,0:T(8,128)(2,1)S(1)}, u32[]{:S(2)}, u32[]{:S(2)}) collective-permute-start(bf16[3,720,128]{2,1,0:T(8,128)(2,1)S(1)} %get-tuple-element.30), channel_id=1, source_target_pairs={{0,1},{1,2},{2,3},{3,4},{4,5},{5,6},{6,7},{7,8},{8,9},{9,10},{10,1... | collective-permute-start | bytes 1658888 | tf_op jit(solution)/shard_map/ppermute | solution.py:44
  526.8 10.8 %collective-permute-start.9 = (bf16[3,720,128]{2,1,0:T(8,128)(2,1)S(1)}, bf16[3,720,128]{2,1,0:T(8,128)(2,1)S(1)}, u32[]{:S(2)}, u32[]{:S(2)}) collective-permute-start(bf16[3,720,128]{2,1,0:T(8,128)(2,1)S(1)} %get-tuple-element.31), channel_id=1, source_target_pairs={{1,0},{2,1},{3,2},{4,3},{5,4},{6,5},{7,6},{8,7},{9,8},{10,9},{11,1... | collective-permute-start | bytes 1658888 | tf_op jit(solution)/shard_map/ppermute | solution.py:45
  537.6 2.8 collective-permute-start.10
  538.7 2.6 collective-permute-start.11
  632.0 31.4 %collective-permute-start.12 = (bf16[3,720,128]{2,1,0:T(8,128)(2,1)}, bf16[3,720,128]{2,1,0:T(8,128)(2,1)S(1)}, u32[]{:S(2)}, u32[]{:S(2)}) collective-permute-start(bf16[3,720,128]{2,1,0:T(8,128)(2,1)} %get-tuple-element.28), channel_id=1, source_target_pairs={{0,1},{1,2},{2,3},{3,4},{4,5},{5,6},{6,7},{7,8},{8,9},{9,10},{10,1... | collective-permute-start | bytes 1658888 | tf_op jit(solution)/shard_map/ppermute | solution.py:44
  635.0 28.4 %collective-permute-start.13 = (bf16[3,720,128]{2,1,0:T(8,128)(2,1)}, bf16[3,720,128]{2,1,0:T(8,128)(2,1)S(1)}, u32[]{:S(2)}, u32[]{:S(2)}) collective-permute-start(bf16[3,720,128]{2,1,0:T(8,128)(2,1)} %get-tuple-element.29), channel_id=1, source_target_pairs={{1,0},{2,1},{3,2},{4,3},{5,4},{6,5},{7,6},{8,7},{9,8},{10,9},{11,1... | collective-permute-start | bytes 1658888 | tf_op jit(solution)/shard_map/ppermute | solution.py:45
  638.2 23.8 %all-to-all-start.5 = ((bf16[128,2,384]{2,1,0:T(2,128)(2,1)}), bf16[128,2,384]{2,1,0:T(2,128)(2,1)}, u32[]{:S(2)}, u32[]{:S(2)}) async-start(bf16[128,2,384]{2,1,0:T(2,128)(2,1)} %copy.87), calls=%async_computation.5 | async-start | bytes 393216 | tf_op jit(solution)/shard_map/all_to_all | solution.py:179
  652.1 244.9 %all-reduce.10.cloned.1.call-start = ((), (), s32[]{:S(2)}) async-start(), calls=%async_computation.8 | async-start | bytes 3407872
  663.5 3.4 collective-permute-start.14
  664.1 2.8 collective-permute-start.15
  (126 other events, 1738.6 us)
Sparse Core Ops, SparseCore 0:
  13.5 147.4 all-reduce.7
  163.3 193.8 all-gather.3
  748.6 148.3 all-reduce.9
where the time goes:
time: 925 us; the launch traced here: 916 us
  waiting for transfers between devices  492 us (53%)
  other arithmetic  207 us (22%)
  matrix products  76.9 us (8%)
  starting transfers between devices  74.6 us (8%)
  local copies, waits for them, and re-layouts  41 us (4%)
  between operations  16.7 us (2%)
    unnamed x5, waiting for transfers between devices  280 us
    all_gather x1, waiting for transfers between devices, collect_rows(): piece = lax.all_gather(values, SEC_TILE, axis=0, tiled=True)  174 us
    add x1, other arithmetic, per_device(): cotangent + depthwise(rims(hidden_adjoint, radius), conv_kernel[layer, ::...  64 us
    mul x1, other arithmetic, per_device(): mask_value[:, :, None] * cotangent  59.1 us
    reduce_sum x2, other arithmetic, cell_forward(): center = hidden - jnp.mean(hidden, axis=-1, keepdims=True)  41.2 us
    dot_general x2, matrix products, cell_backward(): jnp.dot(before_adjoint, expand.T, preferred_element_type=jnp.float32)  29 us
    all_to_all x2, starting transfers between devices, to_bands(): lax.all_to_all(values, SEC_TILE, split_axis=0, concat_axis=1, tiled=True)  27.2 us
    all_to_all x2, starting transfers between devices, turned_blocks(): lax.all_to_all(blocks, axes[k], split_axis=k, concat_axis=k, tiled=True)  19 us
  transfers between devices with their start and end apart: 23, of which 12 were waited for; matrix products, arithmetic and copies ran while one was open for 8% of the time, Pallas kernels for 0%

commit v1 on v0

--- a/solution.py
+++ b/solution.py
@@ -194,7 +194,9 @@
 
 
 def collect_rows(matrix, values, lon_count, fields, offset, half):
-    piece = lax.all_gather(values, SEC_TILE, axis=0, tiled=True)
+    piece = jnp.concatenate(
+        lax.all_to_all(jnp.stack([values] * lax.axis_size(SEC_TILE)), SEC_TILE, 0, 0), axis=0
+    )
     own = lax.dynamic_slice_in_dim(
         piece.reshape(piece.shape[0], lon_count, fields), offset, half, 1
     )

time: 925 us -> 680 us (0.74)
  waiting for transfers between devices: 492 us -> 235 us
  blocking collectives: 8.01 us -> 40.2 us
  starting transfers between devices: 74.6 us -> 59.4 us
    all_gather x1 -> x0, waiting for transfers between devices: 174 us -> none  [collect_rows(): piece = lax.all_gather(values, SEC_TILE, axis=0, tiled=True)]
    unnamed x5 -> x2, waiting for transfers between devices: 280 us -> 162 us
    all_to_all x0 -> x2, waiting for transfers between devices: none -> 30.6 us  [collect_rows(): lax.all_to_all(jnp.stack([values] * lax.axis_size(SEC_TILE)), SEC_TILE, 0...]
    all_to_all x0 -> x2, starting transfers between devices: none -> 21.4 us  [collect_rows(): lax.all_to_all(jnp.stack([values] * lax.axis_size(SEC_TILE)), SEC_TILE, 0...]
    all_to_all x2 -> x1, starting transfers between devices: 27.2 us -> 6.18 us  [to_bands(): lax.all_to_all(values, SEC_TILE, split_axis=0, concat_axis=1, tiled=True)]
    all_to_all x2 -> x3, blocking collectives: 8.01 us -> 24.7 us  [turned_blocks(): lax.all_to_all(blocks, axes[k], split_axis=k, concat_axis=k, tiled=True)]
    all_to_all x0 -> x1, blocking collectives: none -> 15.5 us  [to_bands(): lax.all_to_all(values, SEC_TILE, split_axis=0, concat_axis=1, tiled=True)]
    all_to_all x2 -> x1, starting transfers between devices: 19 us -> 4.74 us  [turned_blocks(): lax.all_to_all(blocks, axes[k], split_axis=k, concat_axis=k, tiled=True)]
  transfers between devices with their start and end apart: 23 -> 21, of which waited for: 12 -> 19; matrix products, arithmetic and copies ran while one was open for 8% -> 5% of each run, Pallas kernels for 0% -> 0%
where the time goes in v1:
time: 680 us; the launch traced here: 673 us
  waiting for transfers between devices  235 us (35%)
  other arithmetic  205 us (30%)
  matrix products  79.2 us (12%)
  starting transfers between devices  59.4 us (9%)
  blocking collectives  40.2 us (6%)
  local copies, waits for them, and re-layouts  38.4 us (6%)
  between operations  16.4 us (2%)
    unnamed x2, waiting for transfers between devices  162 us
    mul x1, other arithmetic, per_device(): mask_value[:, :, None] * cotangent  59.5 us
    add x1, other arithmetic, per_device(): cotangent + depthwise(rims(hidden_adjoint, radius), conv_kernel[layer, ::...  59.3 us
    reduce_sum x2, other arithmetic, cell_forward(): center = hidden - jnp.mean(hidden, axis=-1, keepdims=True)  41.2 us
    all_to_all x2, waiting for transfers between devices, collect_rows(): lax.all_to_all(jnp.stack([values] * lax.axis_size(SEC_TILE)), SEC_TILE, 0...  30.6 us
    dot_general x2, matrix products, cell_backward(): jnp.dot(before_adjoint, expand.T, preferred_element_type=jnp.float32)  29.1 us
    all_to_all x3, blocking collectives, turned_blocks(): lax.all_to_all(blocks, axes[k], split_axis=k, concat_axis=k, tiled=True)  24.7 us
    ppermute x8, waiting for transfers between devices, with_halo(): after = lax.ppermute(first, axis, down)  21.7 us
  transfers between devices with their start and end apart: 21, of which 19 were waited for; matrix products, arithmetic and copies ran while one was open for 5% of the time, Pallas kernels for 0%

profile of v1, /device:TPU:1, one launch (start us, length us, event | category | flops | bytes accessed | tf_op | source)
XLA Modules:
  0.0 673.2 jit_solution(7410057872277585765)
XLA Ops:
  10.5 11.5 %all-to-all-start.3 = ((f32[128,1,2880]{2,1,0:T(1,128)}), f32[128,1,2880]{2,1,0:T(1,128)S(1)}, u32[]{:S(2)}, u32[]{:S(2)}) async-start(f32[128,1,2880]{2,1,0:T(1,128)} %stack.22), calls=%async_computation.3 | async-start | bytes 3014656 | tf_op jit(solution)/shard_map/all_to_all | solution.py:198
  23.1 22.7 %all-to-all-done.3 = f32[128,1,2880]{2,1,0:T(1,128)S(1)} async-done(((f32[128,1,2880]{2,1,0:T(1,128)}), f32[128,1,2880]{2,1,0:T(1,128)S(1)}, u32[]{:S(2)}, u32[]{:S(2)}) %all-to-all-start.3) | async-done | bytes 1474592 | tf_op jit(solution)/shard_map/all_to_all | solution.py:198
  52.4 3.4 collective-permute-start
  59.1 3.5 collective-permute-done
  62.6 4.1 collective-permute-done.1
  72.1 20.6 %fusion.375 = (f32[8,720]{1,0:T(8,128)S(1)}, f32[8,720,128]{2,1,0:T(8,128)S(1)}) fusion(f32[128]{0:T(128)S(1)} %copy-done.69, f32[14,726,128]{2,1,0:T(8,128)S(1)} %maximum_convert_fusion, f32[128]{0:T(128)S(1)} %copy-done.70, f32[128]{0:T(128)S(1)} %copy-done.71, f32[128]{0:T(128)S(1)} %copy-done.72, f32[128]{0:T(128)S(1)} %copy-done.73, ...), kind=kLoop, calls=%fused_computation.842 | loop fusion | flops 72247680 | bytes 147504128 | tf_op jit(solution)/shard_map/reduce_sum | solution.py:80
  96.5 4.9 add_convert_fusion.1
  110.8 4.7 collective-permute-done.5
  121.6 20.6 %fusion.373 = (f32[8,720]{1,0:T(8,128)S(1)}, f32[8,720,128]{2,1,0:T(8,128)S(1)}) fusion(f32[128]{0:T(128)S(1)} %get-tuple-element.135, f32[14,726,128]{2,1,0:T(8,128)S(1)} %maximum_convert_fusion.1, f32[128]{0:T(128)S(1)} %get-tuple-element.136, f32[128]{0:T(128)S(1)} %get-tuple-element.137, f32[128]{0:T(128)S(1)} %get-tuple-element.138, ...), kind=kLoop, calls=%fused_computation.841 | loop fusion | flops 72247680 | bytes 147504128 | tf_op jit(solution)/shard_map/reduce_sum | solution.py:80
  144.1 5.4 fusion.219
  149.5 15.5 %multiply_reduce_fusion.5 = (f32[8,720]{1,0:T(8,128)S(1)}, f32[8,720]{1,0:T(8,128)S(1)}, f32[8,720,128]{2,1,0:T(8,128)}) fusion(f32[128]{0:T(128)S(1)} %get-tuple-element.234, f32[8,720]{1,0:T(8,128)S(1)} %add_rsqrt_fusion, f32[8,720,128]{2,1,0:T(8,128)} %copy-done.1, f32[8,720]{1,0:T(8,128)S(1)} %broadcast_multiply_fusion.6, ...), kind=kOutput, calls=%fused_computation.438 | convolution fusion | flops 1575555840 | bytes 19551744 | tf_op jit(solution)/shard_map/dot_general | solution.py:98
  165.0 6.8 %multiply_convert_fusion.6 = bf16[8,720,128]{2,1,0:T(8,128)(2,1)S(1)} fusion(f32[8,720,128]{2,1,0:T(8,128)} %get-tuple-element.236, f32[8,720,128]{2,1,0:T(8,128)} %copy-done.1, f32[8,720]{1,0:T(8,128)S(1)} %broadcast_multiply_fusion.4, f32[8,720]{1,0:T(8,128)S(1)} %broadcast_multiply_fusion.5, f32[128]{0:T(128)S(1)} %get-tuple-element.234, ...), kind=kLoop, calls=%fused_computation.422 | loop fusion | flops 5898240 | bytes 7465472 | tf_op jit(solution)/shard_map/convert_element_type | solution.py:105
  194.7 4.3 maximum_convert_fusion.2
  199.2 59.3 %convert_add_fusion = f32[8,720,128]{2,1,0:T(8,128)} fusion(bf16[8,720,128]{2,1,0:T(8,128)(2,1)S(1)} %copy-done.14, f32[14,726,128]{2,1,0:T(8,128)} %maximum_convert_fusion.2, f32[128]{0:T(128)} %get-tuple-element.86, f32[128]{0:T(128)} %get-tuple-element.87, f32[128]{0:T(128)} %get-tuple-element.88, f32[128]{0:T(128)} %get-tuple-element.89, ...), kind=kLoop, calls=%fused_computation.26 | loop fusion | flops 72990720 | bytes 148955648 | tf_op jit(solution)/shard_map/add | solution.py:309
  258.6 13.6 %multiply_reduce_fusion.4 = (f32[8,720]{1,0:T(8,128)S(1)}, f32[8,720]{1,0:T(8,128)S(1)}, f32[8,720,128]{2,1,0:T(8,128)}) fusion(f32[128]{0:T(128)S(1)} %get-tuple-element.235, f32[8,720]{1,0:T(8,128)S(1)} %copy-done.22, f32[8,720,128]{2,1,0:T(8,128)S(1)} %get-tuple-element.17, f32[8,720]{1,0:T(8,128)S(1)} %copy-done.16, ...), kind=kOutput, calls=%fused_computation.437 | convolution fusion | flops 1574818560 | bytes 21026304 | tf_op jit(solution)/shard_map/dot_general | solution.py:98
  272.2 7.1 %multiply_convert_fusion.4 = bf16[8,720,128]{2,1,0:T(8,128)(2,1)S(1)} fusion(f32[8,720,128]{2,1,0:T(8,128)} %get-tuple-element.237, f32[8,720,128]{2,1,0:T(8,128)S(1)} %get-tuple-element.17, f32[8,720]{1,0:T(8,128)S(1)} %broadcast_multiply_fusion.2, f32[8,720]{1,0:T(8,128)S(1)} %broadcast_multiply_fusion.3, f32[128]{0:T(128)S(1)} %get-tuple-element.235, ...), kind=kLoop, calls=%fused_computation.419 | loop fusion | flops 5898240 | bytes 7465472 | tf_op jit(solution)/shard_map/convert_element_type | solution.py:105
  290.0 4.1 collective-permute-done.13
  297.7 6.3 collective-permute-done.15
  307.5 59.5 %broadcast_multiply_fusion = (f32[8,720,128]{2,1,0:T(8,128)}, f32[8,720,128]{2,1,0:T(8,128)S(1)}) fusion(f32[8,720]{1,0:T(8,128)S(1)} %copy-done.24, f32[8,720,128]{2,1,0:T(8,128)} %convert_add_fusion, f32[128]{0:T(128)S(1)} %get-tuple-element.37, f32[14,726,128]{2,1,0:T(8,128)} %maximum_convert_fusion.3, f32[128]{0:T(128)S(1)} %get-tuple-element.38, ...), kind=kLoop, calls=%fused_computation.447 | loop fusion | flops 72990720 | bytes 153402368 | tf_op jit(solution)/shard_map/mul | solution.py:313
  367.1 4.5 reduce_sum.115
  375.2 5.0 dynamic_update_slice.7
  386.4 161.7 %all-reduce.5.cloned.1.call-done = (f32[128,360]{1,0:T(8,128)}, f32[128,2880]{1,0:T(8,128)}) async-done(((f32[128,360]{1,0:T(8,128)}, f32[128,2880]{1,0:T(8,128)}), (f32[128,360]{1,0:T(8,128)}, f32[128,2880]{1,0:T(8,128)})) %all-reduce.5.cloned.1.call-update) | async-done | bytes 1658896
  552.0 4.2 all_to_all.48
  556.4 16.1 %all_to_all.49 = bf16[64,2,1,2,384]{4,3,1,2,0:T(2,128)(2,1)S(1)} all-to-all(bf16[64,2,1,2,384]{4,3,1,2,0:T(2,128)(2,1)S(1)} %copy.72), channel_id=1, replica_groups=mesh['sec'=2,'tile_0'=4,'tile_1'=2,'tile_2'=4,'tile_3'=2] {'sec','tile_0..., dimensions={0} | all-to-all | bytes 393216 | tf_op jit(solution)/shard_map/all_to_all | solution.py:27
  577.8 15.5 %all_to_all.50 = bf16[128,2,384]{2,1,0:T(2,128)(2,1)S(1)} all-to-all(bf16[128,2,384]{2,1,0:T(2,128)(2,1)S(1)} %copy.75), channel_id=1, replica_groups=mesh['sec'=2,'tile_0'=4,'tile_1'=2,'tile_2'=4,'tile_3'=2] {'sec','tile_0..., dimensions={0} | all-to-all | bytes 393216 | tf_op jit(solution)/shard_map/all_to_all | solution.py:179
  597.2 4.3 all_to_all.51
  602.3 4.7 all-to-all-start.5
  607.1 9.0 %all-to-all-done.5 = bf16[64,2,1,2,384]{4,3,1,2,0:T(2,128)(2,1)S(1)} async-done(((bf16[64,2,1,2,384]{4,3,1,2,0:T(2,128)(2,1)}), bf16[64,2,1,2,384]{4,3,1,2,0:T(2,128)(2,1)S(1)}, u32[]{:S(2)}, u32[]{:S(2)}) %all-to-all-start.5) | async-done | bytes 196640 | tf_op jit(solution)/shard_map/all_to_all | solution.py:27
  622.3 6.2 all-to-all-start.6
  628.5 8.1 %add_convert_fusion = bf16[8,720,128]{2,1,0:T(8,128)(2,1)} fusion(bf16[8,720,128]{2,1,0:T(8,128)(2,1)} %copy-done.9, f32[8,720,512]{2,1,0:T(8,128)} %fusion.219, f32[8,720]{1,0:T(8,128)S(1)} %copy-done.24, bf16[2,512,128]{2,1,0:T(8,128)(2,1)} %param.35), kind=kOutput, calls=%fused_computation.424 | convolution fusion | flops 784465920 | bytes 14899712 | tf_op jit(solution)/shard_map/dot_general | solution.py:85
  641.5 9.9 %all-to-all-start.7 = ((f32[128,1,360]{2,1,0:T(1,128)}), f32[128,1,360]{2,1,0:T(1,128)}, u32[]{:S(2)}, u32[]{:S(2)}) async-start(f32[128,1,360]{2,1,0:T(1,128)} %stack.26), calls=%async_computation.7 | async-start | bytes 393216 | tf_op jit(solution)/shard_map/all_to_all | solution.py:198
  653.6 7.9 %all-to-all-done.7 = f32[128,1,360]{2,1,0:T(1,128)} async-done(((f32[128,1,360]{2,1,0:T(1,128)}), f32[128,1,360]{2,1,0:T(1,128)}, u32[]{:S(2)}, u32[]{:S(2)}) %all-to-all-start.7) | async-done | bytes 184352 | tf_op jit(solution)/shard_map/all_to_all | solution.py:198
  (355 shorter events, 121.9 us)
Async XLA Ops:
  7.2 568.6 %copy-start = (bf16[1,128,128]{2,1,0:T(8,128)(2,1)S(1)}, bf16[1,128,128]{2,1,0:T(8,128)(2,1)}, u32[]{:S(2)}) copy-start(bf16[1,128,128]{2,1,0:T(8,128)(2,1)} %param.30) | copy-start | bytes 98308
  10.5 35.3 %all-to-all-start.3 = ((f32[128,1,2880]{2,1,0:T(1,128)}), f32[128,1,2880]{2,1,0:T(1,128)S(1)}, u32[]{:S(2)}, u32[]{:S(2)}) async-start(f32[128,1,2880]{2,1,0:T(1,128)} %stack.22), calls=%async_computation.3 | async-start | bytes 3014656 | tf_op jit(solution)/shard_map/all_to_all | solution.py:198
  22.0 526.1 %all-reduce.5.cloned.1.call-start = ((), (), s32[]{:S(2)}) async-start(), calls=%async_computation.8 | async-start | bytes 3407872
  22.0 127.5 %copy-start.23 = (f32[8,720]{1,0:T(8,128)}, f32[8,720]{1,0:T(8,128)S(1)}, u32[]{:S(2)}) copy-start(f32[8,720]{1,0:T(8,128)S(1)} %convert_element_type.219) | copy-start | bytes 69124
  22.3 27.7 %copy-start.30 = (f32[128,8]{0,1:T(8,128)}, f32[128,8]{0,1:T(8,128)S(1)}, u32[]{:S(2)}) copy-start(f32[128,8]{0,1:T(8,128)S(1)} %fusion.336) | copy-start | bytes 12292
  52.4 10.2 %collective-permute-start = (bf16[3,720,128]{2,1,0:T(8,128)(2,1)}, bf16[3,720,128]{2,1,0:T(8,128)(2,1)S(1)}, u32[]{:S(2)}, u32[]{:S(2)}) collective-permute-start(bf16[3,720,128]{2,1,0:T(8,128)(2,1)} %get-tuple-element.34), channel_id=1, source_target_pairs={{0,1},{1,2},{2,3},{3,4},{4,5},{5,6},{6,7},{7,8},{8,9},{9,10},{10,1... | collective-permute-start | bytes 1658888 | tf_op jit(solution)/shard_map/ppermute | solution.py:44
  55.9 10.8 %collective-permute-start.1 = (bf16[3,720,128]{2,1,0:T(8,128)(2,1)S(1)}, bf16[3,720,128]{2,1,0:T(8,128)(2,1)S(1)}, u32[]{:S(2)}, u32[]{:S(2)}) collective-permute-start(bf16[3,720,128]{2,1,0:T(8,128)(2,1)S(1)} %get-tuple-element.35), channel_id=1, source_target_pairs={{1,0},{2,1},{3,2},{4,3},{5,4},{6,5},{7,6},{8,7},{9,8},{10,9},{11,1... | collective-permute-start | bytes 1658888 | tf_op jit(solution)/shard_map/ppermute | solution.py:45
  58.5 47.8 %copy-start.27 = (f32[7,7,128]{2,1,0:T(8,128)}, f32[7,7,128]{2,1,0:T(8,128)S(1)}, u32[]{:S(2)}) copy-start(f32[7,7,128]{2,1,0:T(8,128)S(1)} %bitcast_convert_fusion.1) | copy-start | bytes 75268
  66.7 3.0 collective-permute-start.2
  66.8 3.1 collective-permute-start.3
  101.5 9.3 %collective-permute-start.4 = (bf16[3,720,128]{2,1,0:T(8,128)(2,1)S(1)}, bf16[3,720,128]{2,1,0:T(8,128)(2,1)S(1)}, u32[]{:S(2)}, u32[]{:S(2)}) collective-permute-start(bf16[3,720,128]{2,1,0:T(8,128)(2,1)S(1)} %get-tuple-element.32), channel_id=1, source_target_pairs={{0,1},{1,2},{2,3},{3,4},{4,5},{5,6},{6,7},{7,8},{8,9},{9,10},{10,1... | collective-permute-start | bytes 1658888 | tf_op jit(solution)/shard_map/ppermute | solution.py:44
  104.4 11.1 %collective-permute-start.5 = (bf16[3,720,128]{2,1,0:T(8,128)(2,1)S(1)}, bf16[3,720,128]{2,1,0:T(8,128)(2,1)S(1)}, u32[]{:S(2)}, u32[]{:S(2)}) collective-permute-start(bf16[3,720,128]{2,1,0:T(8,128)(2,1)S(1)} %get-tuple-element.33), channel_id=1, source_target_pairs={{1,0},{2,1},{3,2},{4,3},{5,4},{6,5},{7,6},{8,7},{9,8},{10,9},{11,1... | collective-permute-start | bytes 1658888 | tf_op jit(solution)/shard_map/ppermute | solution.py:45
  115.5 2.7 collective-permute-start.6
  116.9 2.7 collective-permute-start.7
  174.1 13.5 %collective-permute-start.8 = (bf16[3,720,128]{2,1,0:T(8,128)(2,1)}, bf16[3,720,128]{2,1,0:T(8,128)(2,1)S(1)}, u32[]{:S(2)}, u32[]{:S(2)}) collective-permute-start(bf16[3,720,128]{2,1,0:T(8,128)(2,1)} %get-tuple-element.30), channel_id=1, source_target_pairs={{0,1},{1,2},{2,3},{3,4},{4,5},{5,6},{6,7},{7,8},{8,9},{9,10},{10,1... | collective-permute-start | bytes 1658888 | tf_op jit(solution)/shard_map/ppermute | solution.py:44
  177.3 11.1 %collective-permute-start.9 = (bf16[3,720,128]{2,1,0:T(8,128)(2,1)}, bf16[3,720,128]{2,1,0:T(8,128)(2,1)}, u32[]{:S(2)}, u32[]{:S(2)}) collective-permute-start(bf16[3,720,128]{2,1,0:T(8,128)(2,1)} %get-tuple-element.31), channel_id=1, source_target_pairs={{1,0},{2,1},{3,2},{4,3},{5,4},{6,5},{7,6},{8,7},{9,8},{10,9},{11,1... | collective-permute-start | bytes 1658888 | tf_op jit(solution)/shard_map/ppermute | solution.py:45
  189.2 5.4 collective-permute-start.10
  189.3 5.4 collective-permute-start.11
  199.2 59.4 %copy-start.16 = (f32[8,720]{1,0:T(8,128)S(1)}, f32[8,720]{1,0:T(8,128)}, u32[]{:S(2)}) copy-start(f32[8,720]{1,0:T(8,128)} %copy-done.15) | copy-start | bytes 69124
  199.2 59.4 %copy-start.19 = (bf16[2,128,512]{2,1,0:T(8,128)(2,1)S(1)}, bf16[2,128,512]{2,1,0:T(8,128)(2,1)}, u32[]{:S(2)}) copy-start(bf16[2,128,512]{2,1,0:T(8,128)(2,1)} %param.34) | copy-start | bytes 786436
  199.2 59.4 %copy-start.22 = (f32[8,720]{1,0:T(8,128)S(1)}, f32[8,720]{1,0:T(8,128)}, u32[]{:S(2)}) copy-start(f32[8,720]{1,0:T(8,128)} %copy-done.21) | copy-start | bytes 69124
  199.2 59.4 %copy-start.24 = (f32[8,720]{1,0:T(8,128)S(1)}, f32[8,720]{1,0:T(8,128)}, u32[]{:S(2)}) copy-start(f32[8,720]{1,0:T(8,128)} %copy-done.23) | copy-start | bytes 69124
  281.3 8.8 %collective-permute-start.12 = (bf16[3,720,128]{2,1,0:T(8,128)(2,1)}, bf16[3,720,128]{2,1,0:T(8,128)(2,1)S(1)}, u32[]{:S(2)}, u32[]{:S(2)}) collective-permute-start(bf16[3,720,128]{2,1,0:T(8,128)(2,1)} %get-tuple-element.28), channel_id=1, source_target_pairs={{0,1},{1,2},{2,3},{3,4},{4,5},{5,6},{6,7},{7,8},{8,9},{9,10},{10,1... | collective-permute-start | bytes 1658888 | tf_op jit(solution)/shard_map/ppermute | solution.py:44
  283.3 10.8 %collective-permute-start.13 = (bf16[3,720,128]{2,1,0:T(8,128)(2,1)S(1)}, bf16[3,720,128]{2,1,0:T(8,128)(2,1)S(1)}, u32[]{:S(2)}, u32[]{:S(2)}) collective-permute-start(bf16[3,720,128]{2,1,0:T(8,128)(2,1)S(1)} %get-tuple-element.29), channel_id=1, source_target_pairs={{1,0},{2,1},{3,2},{4,3},{5,4},{6,5},{7,6},{8,7},{9,8},{10,9},{11,1... | collective-permute-start | bytes 1658888 | tf_op jit(solution)/shard_map/ppermute | solution.py:45
  294.9 2.8 collective-permute-start.14
  296.4 7.5 %collective-permute-start.15 = (bf16[14,3,128]{2,1,0:T(4,128)(2,1)S(1)}, bf16[14,3,128]{2,1,0:T(4,128)(2,1)S(1)}, u32[]{:S(2)}, u32[]{:S(2)}) collective-permute-start(bf16[14,3,128]{2,1,0:T(4,128)(2,1)S(1)} %get-tuple-element.21), channel_id=1, source_target_pairs={{64,0},{0,64},{65,1},{1,65},{66,2},{2,66},{67,3},{3,67},{68,4},{4,... | collective-permute-start | bytes 32264 | tf_op jit(solution)/shard_map/ppermute | solution.py:45
  380.1 168.7 %copy-start.34 = (f32[384]{0:T(512)S(1)}, f32[384]{0:T(512)}, u32[]{:S(2)}) copy-start(f32[384]{0:T(512)} %param.26) | copy-start | bytes 4612
  384.5 188.1 %copy-start.25 = (bf16[1,128,128]{2,1,0:T(8,128)(2,1)S(1)}, bf16[1,128,128]{2,1,0:T(8,128)(2,1)}, u32[]{:S(2)}) copy-start(bf16[1,128,128]{2,1,0:T(8,128)(2,1)} %param.29) | copy-start | bytes 98308
  385.3 208.0 %copy-start.13 = (bf16[360,128,2]{1,0,2:T(8,128)(2,1)}, bf16[360,128,2]{1,0,2:T(8,128)(2,1)S(1)}, u32[]{:S(2)}) copy-start(bf16[360,128,2]{1,0,2:T(8,128)(2,1)S(1)} %fusion.261) | copy-start | bytes 552964
  602.3 13.7 %all-to-all-start.5 = ((bf16[64,2,1,2,384]{4,3,1,2,0:T(2,128)(2,1)}), bf16[64,2,1,2,384]{4,3,1,2,0:T(2,128)(2,1)S(1)}, u32[]{:S(2)}, u32[]{:S(2)}) async-start(bf16[64,2,1,2,384]{4,3,1,2,0:T(2,128)(2,1)} %copy.84), calls=%async_computation.5 | async-start | bytes 393216 | tf_op jit(solution)/shard_map/all_to_all | solution.py:27
  622.3 16.4 %all-to-all-start.6 = ((bf16[128,2,384]{2,1,0:T(2,128)(2,1)}), bf16[128,2,384]{2,1,0:T(2,128)(2,1)}, u32[]{:S(2)}, u32[]{:S(2)}) async-start(bf16[128,2,384]{2,1,0:T(2,128)(2,1)} %copy.87), calls=%async_computation.6 | async-start | bytes 393216 | tf_op jit(solution)/shard_map/all_to_all | solution.py:179
  641.5 20.0 %all-to-all-start.7 = ((f32[128,1,360]{2,1,0:T(1,128)}), f32[128,1,360]{2,1,0:T(1,128)}, u32[]{:S(2)}, u32[]{:S(2)}) async-start(f32[128,1,360]{2,1,0:T(1,128)} %stack.26), calls=%async_computation.7 | async-start | bytes 393216 | tf_op jit(solution)/shard_map/all_to_all | solution.py:198
  (98 other events, 716.4 us)
Sparse Core Ops, SparseCore 0:
  384.6 163.4 all-reduce.4
